TPU v7x, 128 devices: a whole 4x4x4 slice. The times are simulated.
128 devices in a mesh: dp: 32 (over y, x, z_hi), mp: 4 (over z_lo, core).
Axes of the slice: x: 4, y: 4, z: 4 (z_hi: 2, z_lo: 2; z = z_hi * 2 + z_lo), core: 2. Of those that a mesh axis runs over, the one named last changes fastest.
Arguments:
- page_pool: bfloat16 [2048, 128, 512], P('dp'), may hold values from -6 to 6
- move_count: int32 [32, 32], P('dp'), may hold values from 0 to 2, as said below
- send_slots: int32 [1024, 2], P('dp'), may hold values from 0 to 63, as said below
- page_table: int32 [2048, 16], P('dp'), may hold values from 0 to 127, as said below
- history_len: int32 [2048], P('dp'), may hold values from 1 to 2048, as said below
- queries: bfloat16 [2048, 8, 256], P('dp', 'mp'), may hold values from -6 to 6
- new_entry: bfloat16 [2048, 512], P('dp'), may hold values from -6 to 6
- residual: bfloat16 [2048, 2048], P('dp'), may hold values from -30 to 30
- out_proj: bfloat16 [2048, 2048], P('mp'), may hold values from -0.125 to 0.125
- ffn_gain: float32 [2048], replicated, may hold values from -0.5 to 0.5
- gate_proj: bfloat16 [2048, 16384], P(None, ('dp', 'mp')), may hold values from -0.125 to 0.125
- up_proj: bfloat16 [2048, 16384], P(None, ('dp', 'mp')), may hold values from -0.125 to 0.125
- down_proj: bfloat16 [16384, 2048], P(('dp', 'mp')), may hold values from -0.046875 to 0.046875
Outputs:
- arrived: bfloat16 [2048, 128, 512], P('dp')
- layer_out: bfloat16 [2048, 2048], P('dp')
Inputs may be any that keep to these rules, and one draw needn't show every extreme that they name: `move_count`: zero on the diagonal; in every draw one device receives exactly 2 pages from every other device. `send_slots`: only the first move_count[s, d] entries of row s * 32 + d are sent. `page_table`: for a game of device d, an entry e >= 64 equals 64 + s * 2 + c with c < move_count[s, d]. `history_len`: some game of some device reaches 2048 in every draw.
All inputs are finite; a program needn't handle non-finite values.
Results may differ from a plain program's by a relative error of at most 0.0075.
Values may be sent and summed in bfloat16 or wider, within the bound.
No kernel may reach another device: no remote copies, remote signals or barrier semaphores. Data moves between devices by JAX's collectives and lax.ppermute only.
A program may use at most 128 MiB of HBM per device.

v0:
```python
import math
import jax
import jax.numpy as jnp
from jax import lax
from jax.sharding import PartitionSpec as P


def copy_for_each(array, axis):
    peers = lax.axis_size(axis)
    return lax.all_to_all(
        jnp.broadcast_to(array[None], (peers, *array.shape)), axis, 0, 0, tiled=True
    )


def taken_together(array, axis):
    everything = copy_for_each(array, axis)
    return jnp.sum(everything, axis=0)


def in_blocks(array, dim, peers):
    lengths = array.shape
    tiles = array.reshape(*lengths[:dim], peers, lengths[dim] // peers, *lengths[dim + 1 :])
    return jnp.moveaxis(tiles, dim, 0)


def sum_at_owner(array, axis, dim):
    tiles = in_blocks(array, dim, lax.axis_size(axis))
    arrived = lax.all_to_all(tiles, axis, split_axis=0, concat_axis=0, tiled=True)
    return arrived.astype(jnp.float32).sum(axis=0)


def attend_block(query_blk, page_rows, length_blk, entry_blk):
    head_size = query_blk.shape[-1]
    keys = page_rows[:, :, :head_size]
    values = page_rows[:, :, head_size:]
    factor = 1.0 / math.sqrt(head_size)
    scores = (
        jnp.einsum("bhd,btd->bht", query_blk, keys, preferred_element_type=jnp.float32) * factor
    )
    own = (
        jnp.einsum(
            "bhd,bd->bh", query_blk, entry_blk[:, :head_size], preferred_element_type=jnp.float32
        )
        * factor
    )
    places = jnp.arange(page_rows.shape[1], dtype=jnp.int32)
    valid = places[None, None, :] < length_blk[:, None, None]
    scores = jnp.where(valid, scores, jnp.float32(-1e30))
    biggest = jnp.maximum(jnp.max(scores, axis=-1), own)
    probs = jnp.where(valid, jnp.exp(scores - biggest[..., None]), jnp.float32(0.0))
    prob_own = jnp.exp(own - biggest)
    denom = jnp.sum(probs, axis=-1) + prob_own
    weights = (probs / denom[..., None]).astype(jnp.bfloat16)
    weight_own = (prob_own / denom).astype(jnp.bfloat16)
    result = jnp.einsum("bht,btd->bhd", weights, values, preferred_element_type=jnp.float32)
    result = result + weight_own.astype(jnp.float32)[..., None] * entry_blk[
        :, None, head_size:
    ].astype(jnp.float32)
    return result.astype(jnp.bfloat16)


def local(
    page_pool,
    move_count,
    send_slots,
    page_table,
    history_len,
    queries,
    new_entry,
    residual,
    out_proj,
    ffn_gain,
    gate_proj,
    up_proj,
    down_proj,
):
    senders = lax.axis_size("dp")
    groups = lax.axis_size("mp")
    games = queries.shape[0]
    local_heads = queries.shape[1]
    head_size = queries.shape[2]
    page_len = page_pool.shape[1]
    width = page_pool.shape[2]
    slot_count = send_slots.shape[1]
    table_len = page_table.shape[1]
    live = jnp.arange(slot_count, dtype=jnp.int32)[None, :] < move_count[0][:, None]
    quarter = page_len // groups
    token_part = lax.dynamic_slice_in_dim(page_pool, lax.axis_index("mp") * quarter, quarter, 1)
    outgoing = token_part[send_slots]
    outgoing = jnp.where(live[:, :, None, None], outgoing, jnp.zeros((), jnp.bfloat16))
    partial_pages = lax.all_to_all(outgoing, "dp", split_axis=0, concat_axis=0, tiled=True)
    received = lax.all_gather(partial_pages, "mp", axis=2, tiled=True)
    arrived = received.reshape(senders * slot_count, page_len, width)
    every_page = jnp.concatenate([page_pool, arrived], axis=0)
    block = math.gcd(games, 8)
    table = page_table.reshape(-1, block, table_len)
    lengths = history_len.reshape(-1, block)
    query_dev = queries.reshape(-1, block, local_heads, head_size)
    entry_dev = new_entry.reshape(-1, block, width)

    def one_block(items):
        table_blk, length_blk, query_blk, entry_blk = items
        page_rows = every_page[table_blk].reshape(block, table_len * page_len, width)
        return attend_block(query_blk, page_rows, length_blk, entry_blk)

    attended = lax.map(one_block, (table, lengths, query_dev, entry_dev)).reshape(
        games, local_heads * head_size
    )
    head_part = jnp.dot(attended, out_proj, preferred_element_type=jnp.float32)
    stream_in = residual.astype(jnp.float32) + taken_together(head_part, "mp")
    scale_row = lax.rsqrt(jnp.mean(stream_in * stream_in, axis=-1, keepdims=True) + 1e-06)
    normed = (stream_in * scale_row * (1.0 + ffn_gain)).astype(jnp.bfloat16)
    piece = lax.all_gather(normed, "dp", axis=0, tiled=True)
    gate = jnp.dot(piece, gate_proj, preferred_element_type=jnp.float32)
    up_val = jnp.dot(piece, up_proj, preferred_element_type=jnp.float32)
    hidden = (jax.nn.gelu(gate, approximate=True) * up_val).astype(jnp.bfloat16)
    partial_out = sum_at_owner(
        jnp.dot(hidden, down_proj, preferred_element_type=jnp.float32).astype(jnp.bfloat16), "dp", 0
    )
    mixed = lax.psum(partial_out, "mp")
    layer_out = (stream_in + mixed).astype(jnp.bfloat16)
    return (arrived, layer_out)


def solution(mesh):
    in_specs = (
        P("dp", None, None),
        P("dp", None),
        P("dp", None),
        P("dp", None),
        P("dp"),
        P("dp", "mp", None),
        P("dp", None),
        P("dp", None),
        P("mp", None),
        P(),
        P(None, ("dp", "mp")),
        P(None, ("dp", "mp")),
        P(("dp", "mp"), None),
    )
    out_specs = (P("dp", None, None), P("dp", None))
    return jax.shard_map(local, mesh=mesh, in_specs=in_specs, out_specs=out_specs, check_vma=False)
```

profile of v0, /device:TPU:1, one launch (start us, length us, event | category | flops | bytes accessed | tf_op | source)
XLA Modules:
  0.0 678.5 jit_solution(8073125660301408105)
XLA Ops:
  17.6 40.7 %all_to_all.15 = bf16[32,2,32,512]{3,2,1,0:T(8,128)(2,1)} all-to-all(bf16[32,2,32,512]{3,2,1,0:T(8,128)(2,1)S(1)} %broadcast_select_fusion), channel_id=1, replica_groups=mesh['dp'=32,'mp'=4] {'dp'}, dimensions={0} | all-to-all | bytes 4194304 | tf_op jit(solution)/shard_map/all_to_all | solution.py:91
  58.5 78.7 %all-gather.3.cloned.1.call-done = bf16[32,2,128,512]{3,2,1,0:T(8,128)(2,1)} async-done(((bf16[32,2,32,512]{3,2,1,0:T(8,128)(2,1)}), bf16[32,2,128,512]{3,2,1,0:T(8,128)(2,1)}) %all-gather.3.cloned.1.call-update) | async-done | bytes 8388624 | tf_op jit(solution)/shard_map/all_gather | solution.py:92
  137.2 13.8 %pad_maximum_fusion = bf16[128,128,512]{2,1,0:T(8,128)(2,1)} fusion(bf16[64,128,512]{2,1,0:T(8,128)(2,1)} %bitcast.59, bf16[64,128,512]{2,1,0:T(8,128)(2,1)} %param.15), kind=kLoop, calls=%fused_computation.35 | loop fusion | flops 8388608 | bytes 33554432 | tf_op jit(solution)/shard_map/concatenate | solution.py:94
  150.9 211.9 %while.10 = (s32[]{:T(128)}, bf16[8,8,2,256]{3,2,1,0:T(2,128)(2,1)S(1)}, s32[8,8]{1,0:T(8,128)S(1)}, bf16[8,8,2,256]{3,2,1,0:T(2,128)(2,1)}, s32[8,8,16]{2,1,0:T...) while((s32[]{:T(128)}, bf16[8,8,2,256]{3,2,1,0:T(2,128)(2,1)S(1)}, ...), condition=%wide.region_3.4_spmd, body=%wide.region_0.3_spmd.sunk | while | flops 33922544 | bytes 50886080 | solution.py:106
  151.0 14.1 %gather_fusion = bf16[128,128,512]{2,1,0:T(8,128)(2,1)} fusion(bf16[128,128,512]{2,1,0:T(8,128)(2,1)} %get-tuple-element.136, s32[1024]{0:T(1024)S(1)} %pad_clamp_fusion.3), kind=kCustom, calls=%fused_computation.clone.1 | custom fusion | bytes 33554944 | tf_op jit(solution)/shard_map/while/body/eval_jaxpr/gather | solution.py:103
  165.2 5.8 fusion.71
  177.5 14.0 %gather_fusion = bf16[128,128,512]{2,1,0:T(8,128)(2,1)} fusion(bf16[128,128,512]{2,1,0:T(8,128)(2,1)} %get-tuple-element.136, s32[1024]{0:T(1024)S(1)} %pad_clamp_fusion.3), kind=kCustom, calls=%fused_computation.clone.1 | custom fusion | bytes 33554944 | tf_op jit(solution)/shard_map/while/body/eval_jaxpr/gather | solution.py:103
  191.7 5.8 fusion.71
  204.0 14.1 %gather_fusion = bf16[128,128,512]{2,1,0:T(8,128)(2,1)} fusion(bf16[128,128,512]{2,1,0:T(8,128)(2,1)} %get-tuple-element.136, s32[1024]{0:T(1024)S(1)} %pad_clamp_fusion.3), kind=kCustom, calls=%fused_computation.clone.1 | custom fusion | bytes 33554944 | tf_op jit(solution)/shard_map/while/body/eval_jaxpr/gather | solution.py:103
  218.2 5.8 fusion.71
  230.5 14.0 %gather_fusion = bf16[128,128,512]{2,1,0:T(8,128)(2,1)} fusion(bf16[128,128,512]{2,1,0:T(8,128)(2,1)} %get-tuple-element.136, s32[1024]{0:T(1024)S(1)} %pad_clamp_fusion.3), kind=kCustom, calls=%fused_computation.clone.1 | custom fusion | bytes 33554944 | tf_op jit(solution)/shard_map/while/body/eval_jaxpr/gather | solution.py:103
  257.0 14.1 %gather_fusion = bf16[128,128,512]{2,1,0:T(8,128)(2,1)} fusion(bf16[128,128,512]{2,1,0:T(8,128)(2,1)} %get-tuple-element.136, s32[1024]{0:T(1024)S(1)} %pad_clamp_fusion.3), kind=kCustom, calls=%fused_computation.clone.1 | custom fusion | bytes 33554944 | tf_op jit(solution)/shard_map/while/body/eval_jaxpr/gather | solution.py:103
  271.1 5.8 fusion.71
  283.5 14.1 %gather_fusion = bf16[128,128,512]{2,1,0:T(8,128)(2,1)} fusion(bf16[128,128,512]{2,1,0:T(8,128)(2,1)} %get-tuple-element.136, s32[1024]{0:T(1024)S(1)} %pad_clamp_fusion.3), kind=kCustom, calls=%fused_computation.clone.1 | custom fusion | bytes 33554944 | tf_op jit(solution)/shard_map/while/body/eval_jaxpr/gather | solution.py:103
  297.6 5.8 fusion.71
  310.0 14.0 %gather_fusion = bf16[128,128,512]{2,1,0:T(8,128)(2,1)} fusion(bf16[128,128,512]{2,1,0:T(8,128)(2,1)} %get-tuple-element.136, s32[1024]{0:T(1024)S(1)} %pad_clamp_fusion.3), kind=kCustom, calls=%fused_computation.clone.1 | custom fusion | bytes 33554944 | tf_op jit(solution)/shard_map/while/body/eval_jaxpr/gather | solution.py:103
  336.5 14.1 %gather_fusion = bf16[128,128,512]{2,1,0:T(8,128)(2,1)} fusion(bf16[128,128,512]{2,1,0:T(8,128)(2,1)} %get-tuple-element.136, s32[1024]{0:T(1024)S(1)} %pad_clamp_fusion.3), kind=kCustom, calls=%fused_computation.clone.1 | custom fusion | bytes 33554944 | tf_op jit(solution)/shard_map/while/body/eval_jaxpr/gather | solution.py:103
  369.5 23.6 %all-to-all-done.1 = f32[4,64,2048]{2,1,0:T(8,128)} async-done(((f32[4,64,2048]{2,1,0:T(8,128)}), f32[4,64,2048]{2,1,0:T(8,128)}, u32[]{:S(2)}, u32[]{:S(2)}) %all-to-all-start.1) | async-done | bytes 2097184 | tf_op jit(solution)/shard_map/all_to_all | solution.py:10
  395.9 105.4 %all-gather.5.cloned.1.call-done = bf16[2048,2048]{1,0:T(8,128)(2,1)} async-done(((bf16[64,2048]{1,0:T(8,128)(2,1)}), bf16[2048,2048]{1,0:T(8,128)(2,1)}) %all-gather.5.cloned.1.call-update) | async-done | bytes 8388624 | tf_op jit(solution)/shard_map/all_gather | solution.py:113
  501.3 6.8 %fusion.51 = f32[2048,128]{1,0:T(8,128)} fusion(bf16[2048,2048]{1,0:T(8,128)(2,1)} %all-gather.5.cloned.1.call-done, bf16[2048,128]{1,0:T(8,128)(2,1)} %param.25), kind=kOutput, calls=%fused_computation.69 | convolution fusion | flops 1073741824 | bytes 9961472 | tf_op jit(solution)/shard_map/dot_general | solution.py:114
  508.1 13.2 %convolution_convert_fusion = bf16[2048,2048]{1,0:T(8,128)(2,1)} fusion(bf16[128,2048]{1,0:T(8,128)(2,1)S(1)} %copy-done.2, bf16[2048,2048]{1,0:T(8,128)(2,1)} %all-gather.5.cloned.1.call-done, bf16[2048,128]{1,0:T(8,128)(2,1)} %param.26, f32[2048,128]{1,0:T(8,128)} %fusion.51), kind=kOutput, calls=%fused_computation.37 | convolution fusion | flops 2154299392 | bytes 18874368 | tf_op jit(solution)/shard_map/dot_general | solution.py:118
  521.3 102.2 %all_to_all.16 = bf16[32,64,2048]{2,1,0:T(8,128)(2,1)S(1)} all-to-all(bf16[32,64,2048]{2,1,0:T(8,128)(2,1)} %bitcast.58), channel_id=1, replica_groups=mesh['dp'=32,'mp'=4] {'dp'}, dimensions={0} | all-to-all | bytes 16777216 | tf_op jit(solution)/shard_map/all_to_all | solution.py:28
  626.5 35.9 %all-reduce.2.cloned.1.call-done = f32[64,2048]{1,0:T(8,128)} async-done(((f32[64,2048]{1,0:T(8,128)}), f32[64,2048]{1,0:T(8,128)}) %all-reduce.2.cloned.1.call-update) | async-done | bytes 524304 | tf_op jit(solution)/shard_map/psum | solution.py:120
  664.2 7.8 %copy.39 = bf16[64,128,512]{2,1,0:T(8,128)(2,1)} copy(bf16[64,128,512]{2,1,0:T(8,128)(2,1)} %bitcast.60) | data formatting | bytes 16777216
  (139 shorter events, 95.3 us)
Async XLA Ops:
  7.2 355.8 %copy-start = (bf16[512,2048]{1,0:T(8,128)(2,1)S(1)}, bf16[512,2048]{1,0:T(8,128)(2,1)}, u32[]{:S(2)}) copy-start(bf16[512,2048]{1,0:T(8,128)(2,1)} %param.23) | copy-start | bytes 6291460
  7.2 130.0 %all-gather.3.cloned.1.call-start = ((), (), s32[]{:S(2)}) async-start(), calls=%async_computation.3 | async-start | bytes 10485760 | tf_op jit(solution)/shard_map/all_gather | solution.py:92
  12.2 46.1 %copy-start.3 = (s32[64,16]{0,1:T(8,128)S(1)}, s32[64,16]{0,1:T(8,128)}, u32[]{:S(2)}) copy-start(s32[64,16]{0,1:T(8,128)} %param.18) | copy-start | bytes 12292
  12.2 46.2 %copy-start.5 = (s32[64]{0:T(128)S(1)}, s32[64]{0:T(128)}, u32[]{:S(2)}) copy-start(s32[64]{0:T(128)} %param.19) | copy-start | bytes 772
  362.9 6.6 copy-start.4
  362.9 31.9 %copy-start.1 = (bf16[64,2048]{1,0:T(8,128)(2,1)S(1)}, bf16[64,2048]{1,0:T(8,128)(2,1)}, u32[]{:S(2)}) copy-start(bf16[64,2048]{1,0:T(8,128)(2,1)} %param.22) | copy-start | bytes 786436
  365.0 28.1 %all-to-all-start.1 = ((f32[4,64,2048]{2,1,0:T(8,128)}), f32[4,64,2048]{2,1,0:T(8,128)}, u32[]{:S(2)}, u32[]{:S(2)}) async-start(f32[4,64,2048]{2,1,0:T(8,128)} %broadcast_in_dim.61), calls=%async_computation.1 | async-start | bytes 4194304 | tf_op jit(solution)/shard_map/all_to_all | solution.py:10
  369.4 138.7 %copy-start.2 = (bf16[128,2048]{1,0:T(8,128)(2,1)S(1)}, bf16[128,2048]{1,0:T(8,128)(2,1)}, u32[]{:S(2)}) copy-start(bf16[128,2048]{1,0:T(8,128)(2,1)} %param.27) | copy-start | bytes 1572868
  369.4 131.9 %all-gather.5.cloned.1.call-start = ((), (), s32[]{:S(2)}) async-start(), calls=%async_computation.4 | async-start | bytes 8650752 | tf_op jit(solution)/shard_map/all_gather | solution.py:113
  395.9 266.6 %all-reduce.2.cloned.1.call-start = ((), (), s32[]{:S(2)}) async-start(), calls=%async_computation.5 | async-start | bytes 1048576 | tf_op jit(solution)/shard_map/psum | solution.py:120
Sparse Core Ops, SparseCore 0:
  58.4 78.7 all-gather.2
  396.0 105.2 all-gather.4
  626.6 35.7 all-reduce.1
where the time goes:
time: 681 us; the launch traced here: 679 us
  waiting for transfers between devices  244 us (36%)
  blocking collectives  143 us (21%)
  local copies, waits for them, and re-layouts  135 us (20%)
  matrix products  110 us (16%)
  other arithmetic  27.9 us (4%)
  between operations  13.9 us (2%)
    gather x8, local copies, waits for them, and re-layouts, one_block(): every_page[table_blk].reshape(block, table_len * page_len, width)  112 us
    all_gather x1, waiting for transfers between devices, local(): piece = lax.all_gather(normed, 'dp', axis=0, tiled=True)  105 us
    all_to_all x1, blocking collectives, sum_at_owner(): lax.all_to_all(tiles, axis, split_axis=0, concat_axis=0, tiled=True)  102 us
    all_gather x1, waiting for transfers between devices, local(): received = lax.all_gather(partial_pages, 'mp', axis=2, tiled=True)  78.7 us
    dot_general x8, matrix products, attend_block(): jnp.einsum('bhd,btd->bht', query_blk, keys, preferred_element_type=jnp.fl...  46 us
    all_to_all x1, blocking collectives, local(): lax.all_to_all(outgoing, 'dp', split_axis=0, concat_axis=0, tiled=True)  40.7 us
    dot_general x8, matrix products, attend_block(): jnp.einsum('bht,btd->bhd', weights, values, preferred_element_type=jnp.fl...  37.1 us
    psum x1, waiting for transfers between devices, local(): mixed = lax.psum(partial_out, 'mp')  35.9 us
  transfers between devices with their start and end apart: 4, of which 4 were waited for; matrix products, arithmetic and copies ran while one was open for 0% of the time, Pallas kernels for 0%

commit v1 on v0

--- a/solution.py
+++ b/solution.py
@@ -89,7 +89,9 @@
     outgoing = token_part[send_slots]
     outgoing = jnp.where(live[:, :, None, None], outgoing, jnp.zeros((), jnp.bfloat16))
     partial_pages = lax.all_to_all(outgoing, "dp", split_axis=0, concat_axis=0, tiled=True)
-    received = lax.all_gather(partial_pages, "mp", axis=2, tiled=True)
+    received = jnp.concatenate(
+        lax.all_to_all(jnp.stack([partial_pages] * lax.axis_size("mp")), "mp", 0, 0), axis=2
+    )
     arrived = received.reshape(senders * slot_count, page_len, width)
     every_page = jnp.concatenate([page_pool, arrived], axis=0)
     block = math.gcd(games, 8)

time: 681 us -> 703 us (1.032)
  starting transfers between devices: 4.55 us -> 13.3 us
  waiting for transfers between devices: 244 us -> 252 us
    all_to_all x0 -> x1, waiting for transfers between devices: none -> 92.1 us  [local(): lax.all_to_all(jnp.stack([partial_pages] * lax.axis_size('mp')), 'mp', 0, 0)]
    all_gather x1 -> x0, waiting for transfers between devices: 78.7 us -> none  [local(): received = lax.all_gather(partial_pages, 'mp', axis=2, tiled=True)]
    all_to_all x0 -> x1, local copies, waits for them, and re-layouts: none -> 8.44 us  [local(): lax.all_to_all(jnp.stack([partial_pages] * lax.axis_size('mp')), 'mp', 0, 0)]
    unnamed x15 -> x14, local copies, waits for them, and re-layouts: 7.9 us -> 0.12 us
    all_to_all x0 -> x1, starting transfers between devices: none -> 7.67 us  [local(): lax.all_to_all(jnp.stack([partial_pages] * lax.axis_size('mp')), 'mp', 0, 0)]
where the time goes in v1:
time: 703 us; the launch traced here: 701 us
  waiting for transfers between devices  252 us (36%)
  blocking collectives  143 us (20%)
  local copies, waits for them, and re-layouts  140 us (20%)
  matrix products  110 us (16%)
  other arithmetic  27.9 us (4%)
  between operations  14.1 us (2%)
  starting transfers between devices  13.3 us (2%)
    gather x8, local copies, waits for them, and re-layouts, one_block(): every_page[table_blk].reshape(block, table_len * page_len, width)  112 us
    all_to_all x1, blocking collectives, sum_at_owner(): lax.all_to_all(tiles, axis, split_axis=0, concat_axis=0, tiled=True)  102 us
    all_gather x1, waiting for transfers between devices, local(): piece = lax.all_gather(normed, 'dp', axis=0, tiled=True)  99.4 us
    all_to_all x1, waiting for transfers between devices, local(): lax.all_to_all(jnp.stack([partial_pages] * lax.axis_size('mp')), 'mp', 0, 0)  92.1 us
    dot_general x8, matrix products, attend_block(): jnp.einsum('bhd,btd->bht', query_blk, keys, preferred_element_type=jnp.fl...  46 us
    all_to_all x1, blocking collectives, local(): lax.all_to_all(outgoing, 'dp', split_axis=0, concat_axis=0, tiled=True)  40.6 us
    dot_general x8, matrix products, attend_block(): jnp.einsum('bht,btd->bhd', weights, values, preferred_element_type=jnp.fl...  37.1 us
    psum x1, waiting for transfers between devices, local(): mixed = lax.psum(partial_out, 'mp')  36 us
  transfers between devices with their start and end apart: 4, of which 4 were waited for; matrix products, arithmetic and copies ran while one was open for 0% of the time, Pallas kernels for 0%

profile of v1, /device:TPU:1, one launch (start us, length us, event | category | flops | bytes accessed | tf_op | source)
XLA Modules:
  0.0 700.9 jit_solution(6940298757696859963)
XLA Ops:
  17.5 40.6 %all_to_all.20 = bf16[32,2,32,512]{3,2,1,0:T(8,128)(2,1)S(1)} all-to-all(bf16[32,2,32,512]{3,2,1,0:T(8,128)(2,1)S(1)} %broadcast_select_fusion), channel_id=1, replica_groups=mesh['dp'=32,'mp'=4] {'dp'}, dimensions={0} | all-to-all | bytes 4194304 | tf_op jit(solution)/shard_map/all_to_all | solution.py:91
  62.6 7.7 %all-to-all-start.1 = ((bf16[4,32,2,32,512]{4,3,2,1,0:T(8,128)(2,1)}), bf16[4,32,2,32,512]{4,3,2,1,0:T(8,128)(2,1)}, u32[]{:S(2)}, u32[]{:S(2)}) async-start(bf16[4,32,2,32,512]{4,3,2,1,0:T(8,128)(2,1)} %stack.2), calls=%async_computation.1 | async-start | bytes 16777216 | tf_op jit(solution)/shard_map/all_to_all | solution.py:93
  70.4 92.1 %all-to-all-done.1 = bf16[4,32,2,32,512]{4,3,2,1,0:T(8,128)(2,1)} async-done(((bf16[4,32,2,32,512]{4,3,2,1,0:T(8,128)(2,1)}), bf16[4,32,2,32,512]{4,3,2,1,0:T(8,128)(2,1)}, u32[]{:S(2)}, u32[]{:S(2)}) %all-to-all-start.1) | async-done | bytes 8388640 | tf_op jit(solution)/shard_map/all_to_all | solution.py:93
  162.4 8.4 %copy.25 = bf16[4,32,2,32,512]{4,3,0,2,1:T(8,128)(2,1)} copy(bf16[4,32,2,32,512]{4,3,2,1,0:T(8,128)(2,1)} %all-to-all-done.1) | data formatting | bytes 16777216 | tf_op jit(solution)/shard_map/all_to_all | solution.py:93
  170.9 13.8 %pad_maximum_fusion = bf16[128,128,512]{2,1,0:T(8,128)(2,1)} fusion(bf16[64,128,512]{2,1,0:T(8,128)(2,1)} %bitcast.61, bf16[64,128,512]{2,1,0:T(8,128)(2,1)} %param.15), kind=kLoop, calls=%fused_computation.35 | loop fusion | flops 8388608 | bytes 33554432 | tf_op jit(solution)/shard_map/concatenate | solution.py:96
  184.7 211.9 %while.10 = (s32[]{:T(128)}, bf16[8,8,2,256]{3,2,1,0:T(2,128)(2,1)S(1)}, s32[8,8]{1,0:T(8,128)S(1)}, bf16[8,8,2,256]{3,2,1,0:T(2,128)(2,1)}, s32[8,8,16]{2,1,0:T...) while((s32[]{:T(128)}, bf16[8,8,2,256]{3,2,1,0:T(2,128)(2,1)S(1)}, ...), condition=%wide.region_3.4_spmd, body=%wide.region_0.3_spmd.sunk | while | flops 33922544 | bytes 50886080 | solution.py:108
  184.8 14.1 %gather_fusion = bf16[128,128,512]{2,1,0:T(8,128)(2,1)} fusion(bf16[128,128,512]{2,1,0:T(8,128)(2,1)} %get-tuple-element.136, s32[1024]{0:T(1024)S(1)} %pad_clamp_fusion.3), kind=kCustom, calls=%fused_computation.clone.1 | custom fusion | bytes 33554944 | tf_op jit(solution)/shard_map/while/body/eval_jaxpr/gather | solution.py:105
  198.9 5.8 fusion.71
  211.3 14.0 %gather_fusion = bf16[128,128,512]{2,1,0:T(8,128)(2,1)} fusion(bf16[128,128,512]{2,1,0:T(8,128)(2,1)} %get-tuple-element.136, s32[1024]{0:T(1024)S(1)} %pad_clamp_fusion.3), kind=kCustom, calls=%fused_computation.clone.1 | custom fusion | bytes 33554944 | tf_op jit(solution)/shard_map/while/body/eval_jaxpr/gather | solution.py:105
  225.4 5.8 fusion.71
  237.7 14.1 %gather_fusion = bf16[128,128,512]{2,1,0:T(8,128)(2,1)} fusion(bf16[128,128,512]{2,1,0:T(8,128)(2,1)} %get-tuple-element.136, s32[1024]{0:T(1024)S(1)} %pad_clamp_fusion.3), kind=kCustom, calls=%fused_computation.clone.1 | custom fusion | bytes 33554944 | tf_op jit(solution)/shard_map/while/body/eval_jaxpr/gather | solution.py:105
  264.2 14.0 %gather_fusion = bf16[128,128,512]{2,1,0:T(8,128)(2,1)} fusion(bf16[128,128,512]{2,1,0:T(8,128)(2,1)} %get-tuple-element.136, s32[1024]{0:T(1024)S(1)} %pad_clamp_fusion.3), kind=kCustom, calls=%fused_computation.clone.1 | custom fusion | bytes 33554944 | tf_op jit(solution)/shard_map/while/body/eval_jaxpr/gather | solution.py:105
  278.4 5.8 fusion.71
  290.7 14.1 %gather_fusion = bf16[128,128,512]{2,1,0:T(8,128)(2,1)} fusion(bf16[128,128,512]{2,1,0:T(8,128)(2,1)} %get-tuple-element.136, s32[1024]{0:T(1024)S(1)} %pad_clamp_fusion.3), kind=kCustom, calls=%fused_computation.clone.1 | custom fusion | bytes 33554944 | tf_op jit(solution)/shard_map/while/body/eval_jaxpr/gather | solution.py:105
  304.9 5.8 fusion.71
  317.2 14.1 %gather_fusion = bf16[128,128,512]{2,1,0:T(8,128)(2,1)} fusion(bf16[128,128,512]{2,1,0:T(8,128)(2,1)} %get-tuple-element.136, s32[1024]{0:T(1024)S(1)} %pad_clamp_fusion.3), kind=kCustom, calls=%fused_computation.clone.1 | custom fusion | bytes 33554944 | tf_op jit(solution)/shard_map/while/body/eval_jaxpr/gather | solution.py:105
  343.7 14.0 %gather_fusion = bf16[128,128,512]{2,1,0:T(8,128)(2,1)} fusion(bf16[128,128,512]{2,1,0:T(8,128)(2,1)} %get-tuple-element.136, s32[1024]{0:T(1024)S(1)} %pad_clamp_fusion.3), kind=kCustom, calls=%fused_computation.clone.1 | custom fusion | bytes 33554944 | tf_op jit(solution)/shard_map/while/body/eval_jaxpr/gather | solution.py:105
  370.2 14.1 %gather_fusion = bf16[128,128,512]{2,1,0:T(8,128)(2,1)} fusion(bf16[128,128,512]{2,1,0:T(8,128)(2,1)} %get-tuple-element.136, s32[1024]{0:T(1024)S(1)} %pad_clamp_fusion.3), kind=kCustom, calls=%fused_computation.clone.1 | custom fusion | bytes 33554944 | tf_op jit(solution)/shard_map/while/body/eval_jaxpr/gather | solution.py:105
  404.1 24.8 %all-to-all-done.2 = f32[4,64,2048]{2,1,0:T(8,128)} async-done(((f32[4,64,2048]{2,1,0:T(8,128)}), f32[4,64,2048]{2,1,0:T(8,128)}, u32[]{:S(2)}, u32[]{:S(2)}) %all-to-all-start.2) | async-done | bytes 2097184 | tf_op jit(solution)/shard_map/all_to_all | solution.py:10
  431.9 99.4 %all-gather.2.cloned.1.call-done = bf16[2048,2048]{1,0:T(8,128)(2,1)} async-done(((bf16[64,2048]{1,0:T(8,128)(2,1)}), bf16[2048,2048]{1,0:T(8,128)(2,1)}) %all-gather.2.cloned.1.call-update) | async-done | bytes 8388624 | tf_op jit(solution)/shard_map/all_gather | solution.py:115
  531.3 6.8 fusion.51
  538.1 13.1 %convolution_convert_fusion = bf16[2048,2048]{1,0:T(8,128)(2,1)} fusion(bf16[128,2048]{1,0:T(8,128)(2,1)S(1)} %copy-done.2, bf16[2048,2048]{1,0:T(8,128)(2,1)} %all-gather.2.cloned.1.call-done, bf16[2048,128]{1,0:T(8,128)(2,1)} %param.26, f32[2048,128]{1,0:T(8,128)} %fusion.51), kind=kOutput, calls=%fused_computation.37 | convolution fusion | flops 2154299392 | bytes 18874368 | tf_op jit(solution)/shard_map/dot_general | solution.py:120
  551.2 102.2 %all_to_all.21 = bf16[32,64,2048]{2,1,0:T(8,128)(2,1)S(1)} all-to-all(bf16[32,64,2048]{2,1,0:T(8,128)(2,1)} %bitcast.60), channel_id=1, replica_groups=mesh['dp'=32,'mp'=4] {'dp'}, dimensions={0} | all-to-all | bytes 16777216 | tf_op jit(solution)/shard_map/all_to_all | solution.py:28
  656.3 36.0 %all-reduce.2.cloned.1.call-done = f32[64,2048]{1,0:T(8,128)} async-done(((f32[64,2048]{1,0:T(8,128)}), f32[64,2048]{1,0:T(8,128)}) %all-reduce.2.cloned.1.call-update) | async-done | bytes 524304 | tf_op jit(solution)/shard_map/psum | solution.py:122
  (139 shorter events, 106.5 us)
Async XLA Ops:
  7.2 389.5 %copy-start = (bf16[512,2048]{1,0:T(8,128)(2,1)S(1)}, bf16[512,2048]{1,0:T(8,128)(2,1)}, u32[]{:S(2)}) copy-start(bf16[512,2048]{1,0:T(8,128)(2,1)} %param.23) | copy-start | bytes 6291460
  62.6 7.7 %copy-start.3 = (s32[64,16]{0,1:T(8,128)S(1)}, s32[64,16]{0,1:T(8,128)}, u32[]{:S(2)}) copy-start(s32[64,16]{0,1:T(8,128)} %param.18) | copy-start | bytes 12292
  62.6 7.8 %copy-start.5 = (s32[64]{0:T(128)S(1)}, s32[64]{0:T(128)}, u32[]{:S(2)}) copy-start(s32[64]{0:T(128)} %param.19) | copy-start | bytes 772
  62.6 99.9 %all-to-all-start.1 = ((bf16[4,32,2,32,512]{4,3,2,1,0:T(8,128)(2,1)}), bf16[4,32,2,32,512]{4,3,2,1,0:T(8,128)(2,1)}, u32[]{:S(2)}, u32[]{:S(2)}) async-start(bf16[4,32,2,32,512]{4,3,2,1,0:T(8,128)(2,1)} %stack.2), calls=%async_computation.1 | async-start | bytes 16777216 | tf_op jit(solution)/shard_map/all_to_all | solution.py:93
  396.6 7.5 %copy-start.4 = (f32[2048]{0:T(1024)S(1)}, f32[2048]{0:T(1024)}, u32[]{:S(2)}) copy-start(f32[2048]{0:T(1024)} %param.24) | copy-start | bytes 24580
  396.6 34.0 %copy-start.1 = (bf16[64,2048]{1,0:T(8,128)(2,1)S(1)}, bf16[64,2048]{1,0:T(8,128)(2,1)}, u32[]{:S(2)}) copy-start(bf16[64,2048]{1,0:T(8,128)(2,1)} %param.22) | copy-start | bytes 786436
  398.7 30.2 %all-to-all-start.2 = ((f32[4,64,2048]{2,1,0:T(8,128)}), f32[4,64,2048]{2,1,0:T(8,128)}, u32[]{:S(2)}, u32[]{:S(2)}) async-start(f32[4,64,2048]{2,1,0:T(8,128)} %broadcast_in_dim.61), calls=%async_computation.2 | async-start | bytes 4194304 | tf_op jit(solution)/shard_map/all_to_all | solution.py:10
  404.1 134.0 %copy-start.2 = (bf16[128,2048]{1,0:T(8,128)(2,1)S(1)}, bf16[128,2048]{1,0:T(8,128)(2,1)}, u32[]{:S(2)}) copy-start(bf16[128,2048]{1,0:T(8,128)(2,1)} %param.27) | copy-start | bytes 1572868
  404.1 127.2 %all-gather.2.cloned.1.call-start = ((), (), s32[]{:S(2)}) async-start(), calls=%async_computation.4 | async-start | bytes 8650752 | tf_op jit(solution)/shard_map/all_gather | solution.py:115
  431.7 260.6 %all-reduce.2.cloned.1.call-start = ((), (), s32[]{:S(2)}) async-start(), calls=%async_computation.5 | async-start | bytes 1048576 | tf_op jit(solution)/shard_map/psum | solution.py:122
Sparse Core Ops, SparseCore 0:
  431.8 99.4 all-gather.1
  656.4 35.8 all-reduce.1
